TPU v7x, 512 devices: a 8x2x16 block of a 8x8x16 slice. The times are simulated.
512 devices in a mesh: groups: 2 (over y), range: 128 (over z, x), sub: 2 (over core).
Axes of the slice: x: 8, y: 2, z: 16, core: 2. Of those that a mesh axis runs over, the one named last changes fastest.
The devices are a block of a 8x8x16 slice.
Arguments:
- samples: float32 [2, 1024, 512, 128], P(None, ('groups', 'range', 'sub')), parts along dimension 1, may hold values from -6 to 6
- beam_weights: float32 [512, 8, 2, 64, 128], P(('groups', 'range'), None, None, None, 'sub'), parts along dimension 0, may hold values from -0.25 to 0.25
- subarrays: int32 [512, 8, 64], P(('groups', 'range', 'sub')), parts along dimension 0, may hold values from 0 to 511, as said below
- training: int32 [1024], P(('groups', 'range', 'sub')), parts along dimension 0, may hold values 0 or 1
Outputs:
- covariance: float32 [512, 8, 64, 128], P(('groups', 'range', 'sub')), parts along dimension 0
- filtered: float32 [2, 128, 1024, 128], P(None, None, ('groups', 'range', 'sub')), parts along dimension 2
- energy: float32 [256], P('groups'), parts along dimension 0
There are 2 independent parts, one for each index of `groups`. A program takes and returns all parts, laid end to end along the dimension named above; each array names one. Nothing has to cross between parts.
Inputs may be any that keep to these rules, and one draw needn't show every extreme that they name: `subarrays`: in each gate block the 512 indices are all 512 channels, each once.
All inputs are finite; a program needn't handle non-finite values. No bound on the sum of `training` on one device may be relied on, other than what follows from the above.
Results may differ from a plain program's by a relative error of at most 0.0003.
Values sent between devices are 32-bit elements; how exact they have to be, the bound alone decides.
A program may use at most 64 MiB of HBM per device.

v0:
```python
import functools
import jax
import jax.numpy as jnp
from jax import lax
from jax.sharding import Mesh
from jax.sharding import PartitionSpec as P

GB = 2
RANGE = ("range_0", "range_1")
RANGE_SUB = ("range_0", "range_1", "sub")
GROUPS_RANGE_SUB = ("groups", "range_0", "range_1", "sub")
GROUPS_RANGE = ("groups", "range_0", "range_1")
loading = 0.05


def split_up(array, dim, peers):
    lengths = array.shape
    parts = array.reshape(*lengths[:dim], peers, lengths[dim] // peers, *lengths[dim + 1 :])
    return jnp.moveaxis(parts, dim, 0)


def joined_along(parts, dim):
    lengths = list(parts.shape[1:])
    lengths[dim] *= parts.shape[0]
    return jnp.moveaxis(parts, 0, dim).reshape(lengths)


def one_exchange(array, axis, axes, splits, concats):
    sizes = [lax.axis_size(a) for a in axes]
    parts = split_up(array, splits[0], sizes[0])
    parts = jnp.moveaxis(split_up(parts, splits[1] + 1, sizes[1]), 0, 1)
    inside = parts.shape[2:]
    parts = parts.reshape(-1, *inside)
    parts = lax.all_to_all(parts, axis, split_axis=0, concat_axis=0, tiled=True)
    parts = joined_along(parts.reshape(*sizes, *inside), concats[0] + 1)
    return joined_along(parts, concats[1])


def by_axis(array, axes):
    return functools.reduce(lax.psum, axes, array)


def block_terms(snaps, chosen, weights, masked, factor):
    highest = lax.Precision.HIGHEST
    picked = jnp.take(snaps, chosen, axis=1)
    real_part = picked[0]
    imag_part = picked[1]
    real_masked = real_part * masked
    imag_masked = imag_part * masked
    cov_real = (
        jnp.einsum("snx,smx->snm", real_masked, real_part, precision=highest)
        + jnp.einsum("snx,smx->snm", imag_masked, imag_part, precision=highest)
    ) * factor
    cov_imag = (
        jnp.einsum("snx,smx->snm", imag_masked, real_part, precision=highest)
        - jnp.einsum("snx,smx->snm", real_masked, imag_part, precision=highest)
    ) * factor
    w_real = weights[:, 0]
    w_imag = weights[:, 1]
    out_real = jnp.einsum("snk,snx->kx", w_real, real_part, precision=highest) + jnp.einsum(
        "snk,snx->kx", w_imag, imag_part, precision=highest
    )
    out_imag = jnp.einsum("snk,snx->kx", w_real, imag_part, precision=highest) - jnp.einsum(
        "snk,snx->kx", w_imag, real_part, precision=highest
    )
    prod_real = jnp.einsum("snm,smk->snk", cov_real, w_real, precision=highest) - jnp.einsum(
        "snm,smk->snk", cov_imag, w_imag, precision=highest
    )
    prod_imag = jnp.einsum("snm,smk->snk", cov_real, w_imag, precision=highest) + jnp.einsum(
        "snm,smk->snk", cov_imag, w_real, precision=highest
    )
    quadratic = jnp.sum(w_real * prod_real + w_imag * prod_imag, axis=(0, 1))
    inverse = 1.0 / jnp.sqrt(quadratic + loading)
    filtered = jnp.stack([out_real * inverse[:, None], out_imag * inverse[:, None]])
    energy = jnp.sum(out_real * out_real + out_imag * out_imag, axis=1)
    covariance = jnp.concatenate([cov_real, cov_imag], axis=-1)
    return (covariance, filtered, energy)


def body(samples, beam_weights, subarrays, training):
    range_count = lax.axis_size(RANGE)
    core_count = lax.axis_size("sub")
    parts_iq, chan_dev, all_gates, pulses = samples.shape
    gate_dev = all_gates // (range_count * core_count)
    channels = chan_dev * range_count * core_count
    blocks_dev = gate_dev // GB
    spread = samples.reshape(parts_iq, 1, 1, chan_dev, range_count, core_count, gate_dev, pulses)
    turned = one_exchange(spread, RANGE_SUB, (RANGE, "sub"), (4, 5), (1, 2))
    local_data = turned.reshape(parts_iq, channels, blocks_dev, GB * pulses).transpose(2, 0, 1, 3)
    mine = lax.all_to_all(beam_weights, "sub", split_axis=0, concat_axis=4, tiled=True)
    gates_on = training.astype(jnp.float32).reshape(blocks_dev, GB)
    masked = jnp.repeat(gates_on, pulses, axis=1)
    factor = 1.0 / (GB * pulses)
    covs, filts, energies = jax.vmap(block_terms, in_axes=(0, 0, 0, 0, None))(
        local_data, subarrays, mine, masked, factor
    )
    beams = filts.shape[2]
    filtered = filts.reshape(blocks_dev, parts_iq, beams, GB, pulses).transpose(1, 2, 0, 3, 4)
    filtered = filtered.reshape(parts_iq, beams, gate_dev, pulses)
    total = by_axis(jnp.sum(energies, axis=0), RANGE_SUB)
    energy = total / (all_gates * pulses)
    return (covs, filtered, energy)


def solution(mesh):
    torus = Mesh(
        mesh.devices.reshape(mesh.shape["groups"], 16, 8, mesh.shape["sub"]),
        ("groups", "range_0", "range_1", "sub"),
    )
    placed = (
        P(None, GROUPS_RANGE_SUB, None, None),
        P(GROUPS_RANGE, None, None, None, "sub"),
        P(GROUPS_RANGE_SUB, None, None),
        P(GROUPS_RANGE_SUB),
    )
    return jax.shard_map(
        body,
        mesh=torus,
        in_specs=placed,
        out_specs=(
            P(GROUPS_RANGE_SUB, None, None, None),
            P(None, None, GROUPS_RANGE_SUB, None),
            P("groups"),
        ),
        check_vma=False,
    )
```

profile of v0, /device:TPU:65, one launch (start us, length us, event | category | flops | bytes accessed | tf_op | source)
XLA Modules:
  0.0 181.8 jit_solution(4154683008116402408)
XLA Ops:
  0.6 0.0 copy-start
  0.6 2.5 %reshape.168 = f32[2,1,65536]{2,1,0:T(1,128)} reshape(f32[2,8,2,64,64]{4,3,2,1,0:T(8,128)} %param.5) | data formatting | bytes 1048576
  3.2 44.9 %all-to-all-start.1 = ((f32[2,1,65536]{2,1,0:T(1,128)}), f32[2,1,65536]{2,1,0:T(1,128)S(1)}, u32[]{:S(2)}, u32[]{:S(2)}) async-start(f32[2,1,65536]{2,1,0:T(1,128)} %reshape.168), calls=%async_computation.1 | async-start | bytes 1048576 | tf_op jit(solution)/shard_map/all_to_all | solution.py:90
  48.1 0.0 copy-done
  48.1 1.3 copy.16
  49.4 0.0 all-to-all-done.1
  49.4 0.0 copy-start.2
  49.5 0.0 copy-start.1
  49.5 16.2 %all-to-all-start = ((f32[256,2,1,1,2,1,1,2,128]{8,7,4,1,6,5,3,2,0:T(2,128)}), f32[256,2,1,1,2,1,1,2,128]{8,7,4,1,6,5,3,2,0:T(2,128)S(1)}, u32[]{:S(2)}, u32[]{:S(2)}) async-start(f32[256,2,1,1,2,1,1,2,128]{8,7,4,1,6,5,3,2,0:T(2,128)} %bitcast.5), calls=%async_computation | async-start | bytes 2097152 | tf_op jit(solution)/shard_map/all_to_all | solution.py:34
  65.7 0.0 copy-done.2
  65.7 0.0 copy-done.1
  65.7 0.1 reshape.158
  65.8 0.5 broadcast.75
  66.3 2.3 %reduce.5 = f32[2,65536]{1,0:T(2,128)S(1)} reduce(f32[2,1,65536]{2,1,0:T(1,128)S(1)} %all-to-all-done.1, f32[]{:T(128)} %broadcast.75), dimensions={1}, to_apply=%all_to_all.17.reduce_sub_computation | reduce | bytes 1048580 | tf_op jit(solution)/shard_map/all_to_all | solution.py:90
  68.6 0.6 reshape.169
  69.3 1.9 %copy.20 = f32[1,8,2,64,2,64]{5,4,3,1,2,0:T(2,128)} copy(f32[1,8,2,64,2,64]{5,3,2,1,4,0:T(8,128)S(1)} %bitcast.104) | data formatting | bytes 1048576 | tf_op jit(solution)/shard_map/all_to_all | solution.py:90
  71.1 1.8 all_to_all.20
  72.9 0.1 broadcast_bitcast_fusion
  73.0 48.2 %all-to-all-done = f32[256,2,1,1,2,1,1,2,128]{8,7,4,1,6,5,3,2,0:T(2,128)S(1)} async-done(((f32[256,2,1,1,2,1,1,2,128]{8,7,4,1,6,5,3,2,0:T(2,128)}), f32[256,2,1,1,2,1,1,2,128]{8,7,4,1,6,5,3,2,0:T(2,128)S(1)}, u32[]{:S(2)}, u32[]{:S(2)}) %all-to-all-start) | async-done | bytes 1048608 | tf_op jit(solution)/shard_map/all_to_all | solution.py:34
  121.3 0.4 copy.17
  121.6 0.8 copy.18
  122.4 2.6 %gather_fusion = f32[512,2,256]{2,1,0:T(2,128)S(1)} fusion(f32[1,2,512,256]{3,1,2,0:T(2,128)S(1)} %copy.18, s32[512]{0:T(512)S(1)} %reshape.158), kind=kCustom, calls=%fused_computation | custom fusion | bytes 2101248 | tf_op jit(solution)/shard_map/vmap(jit(_take))/gather | solution.py:45
  125.0 0.1 copy.19
  125.1 0.1 broadcast_select_fusion
  125.2 1.0 convolution_bitcast_fusion.2
  126.2 1.0 convolution_bitcast_fusion
  127.2 0.6 fusion.12
  127.9 0.6 fusion.2
  128.5 0.4 fusion.19
  128.9 0.4 fusion.18
  129.3 0.6 fusion.8
  129.9 1.0 fusion.6
  130.9 0.6 fusion.3
  131.6 0.4 fusion
  132.0 0.4 fusion.5
  132.4 1.0 add_reduce_fusion
  133.5 20.4 %psum.21 = f32[128]{0:T(128)S(1)} all-reduce(f32[128]{0:T(128)S(1)} %get-tuple-element.3), channel_id=1, replica_groups=mesh['groups'=2,'range_0'=16,'range_1'=8,'sub'=2] {'range_0'}, use_global_device_ids=true, to_apply=%region_2.3 | all-reduce | flops 128 | bytes 1024 | tf_op jit(solution)/shard_map/psum | solution.py:40
  153.8 11.9 %psum.22 = f32[128]{0:T(128)S(1)} all-reduce(f32[128]{0:T(128)S(1)} %psum.21), channel_id=1, replica_groups=mesh['groups'=2,'range_0'=16,'range_1'=8,'sub'=2] {'range_1'}, use_global_device_ids=true, to_apply=%region_3.4 | all-reduce | flops 128 | bytes 1024 | tf_op jit(solution)/shard_map/psum | solution.py:40
  165.7 13.7 %psum.23 = f32[128]{0:T(128)S(1)} all-reduce(f32[128]{0:T(128)S(1)} %psum.22), channel_id=1, replica_groups=mesh['groups'=2,'range_0'=16,'range_1'=8,'sub'=2] {'sub'}, use_global_device_ids=true, to_apply=%region_4.5 | all-reduce | flops 128 | bytes 1024 | tf_op jit(solution)/shard_map/psum | solution.py:40
  179.4 0.5 broadcast_multiply_fusion.2
  179.9 0.1 copy.21
  180.0 0.1 copy.22
  180.2 0.8 pad_maximum_fusion
  181.0 0.8 pad_maximum_fusion.1
  (6 shorter events, 0.0 us)
Async XLA Ops:
  0.6 47.4 %copy-start = (f32[2,2,512,128]{3,2,1,0:T(8,128)S(1)}, f32[2,2,512,128]{3,2,1,0:T(8,128)}, u32[]{:S(2)}) copy-start(f32[2,2,512,128]{3,2,1,0:T(8,128)} %param.4) | copy-start | bytes 3145732
  3.2 46.3 %all-to-all-start.1 = ((f32[2,1,65536]{2,1,0:T(1,128)}), f32[2,1,65536]{2,1,0:T(1,128)S(1)}, u32[]{:S(2)}, u32[]{:S(2)}) async-start(f32[2,1,65536]{2,1,0:T(1,128)} %reshape.168), calls=%async_computation.1 | async-start | bytes 1048576 | tf_op jit(solution)/shard_map/all_to_all | solution.py:90
  49.4 16.2 %copy-start.2 = (s32[2]{0:T(128)S(1)}, s32[2]{0:T(128)}, u32[]{:S(2)}) copy-start(s32[2]{0:T(128)} %param.7) | copy-start | bytes 28
  49.5 16.2 %copy-start.1 = (s32[1,8,64]{2,1,0:T(8,128)S(1)}, s32[1,8,64]{2,1,0:T(8,128)}, u32[]{:S(2)}) copy-start(s32[1,8,64]{2,1,0:T(8,128)} %param.6) | copy-start | bytes 6148
  49.5 71.8 %all-to-all-start = ((f32[256,2,1,1,2,1,1,2,128]{8,7,4,1,6,5,3,2,0:T(2,128)}), f32[256,2,1,1,2,1,1,2,128]{8,7,4,1,6,5,3,2,0:T(2,128)S(1)}, u32[]{:S(2)}, u32[]{:S(2)}) async-start(f32[256,2,1,1,2,1,1,2,128]{8,7,4,1,6,5,3,2,0:T(2,128)} %bitcast.5), calls=%async_computation | async-start | bytes 2097152 | tf_op jit(solution)/shard_map/all_to_all | solution.py:34
where the time goes:
time: 182 us
  starting transfers between devices  61.1 us (34%)
  waiting for transfers between devices  48.3 us (27%)
  blocking collectives  46 us (25%)
  local copies, waits for them, and re-layouts  12.9 us (7%)
  matrix products  8.12 us (4%)
  other arithmetic  4.67 us (3%)
    all_to_all x1, waiting for transfers between devices, one_exchange(): parts = lax.all_to_all(parts, axis, split_axis=0, concat_axis=0, tiled=True)  48.2 us
    psum x3, blocking collectives, by_axis(): return functools.reduce(lax.psum, axes, array)  46 us
    all_to_all x1, starting transfers between devices, body(): lax.all_to_all(beam_weights, 'sub', split_axis=0, concat_axis=4, tiled=True)  44.9 us
    all_to_all x1, starting transfers between devices, one_exchange(): parts = lax.all_to_all(parts, axis, split_axis=0, concat_axis=0, tiled=True)  16.2 us
    all_to_all x3, local copies, waits for them, and re-layouts, body(): lax.all_to_all(beam_weights, 'sub', split_axis=0, concat_axis=4, tiled=True)  4.18 us
  transfers between devices with their start and end apart: 2, of which 1 were waited for; matrix products, arithmetic and copies ran while one was open for 4% of the time, Pallas kernels for 0%

commit v1 on v0

--- a/solution.py
+++ b/solution.py
@@ -87,7 +87,12 @@
     spread = samples.reshape(parts_iq, 1, 1, chan_dev, range_count, core_count, gate_dev, pulses)
     turned = one_exchange(spread, RANGE_SUB, (RANGE, "sub"), (4, 5), (1, 2))
     local_data = turned.reshape(parts_iq, channels, blocks_dev, GB * pulses).transpose(2, 0, 1, 3)
-    mine = lax.all_to_all(beam_weights, "sub", split_axis=0, concat_axis=4, tiled=True)
+    mine = jnp.concatenate(
+        lax.all_to_all(
+            jnp.stack(jnp.split(beam_weights, lax.axis_size("sub"), axis=0)), "sub", 0, 0
+        ),
+        axis=4,
+    )
     gates_on = training.astype(jnp.float32).reshape(blocks_dev, GB)
     masked = jnp.repeat(gates_on, pulses, axis=1)
     factor = 1.0 / (GB * pulses)

time: 182 us -> 181 us (level)
    all_to_all x3 -> x1, local copies, waits for them, and re-layouts: 4.18 us -> 0.51 us  [body(): lax.all_to_all(jnp.stack(jnp.split(beam_weights, lax.axis_size('sub'), ax...]
    reshape x0 -> x2, local copies, waits for them, and re-layouts: none -> 3.67 us  [body(): jnp.concatenate(lax.all_to_all(jnp.stack(jnp.split(beam_weights, lax.axis...]
  transfers between devices with their start and end apart: 2 -> 2, of which waited for: 1 -> 1; matrix products, arithmetic and copies ran while one was open for 4% -> 5% of each run, Pallas kernels for 0% -> 0%
where the time goes in v1:
time: 181 us
  starting transfers between devices  61.1 us (34%)
  waiting for transfers between devices  47.7 us (26%)
  blocking collectives  46 us (25%)
  local copies, waits for them, and re-layouts  13.5 us (7%)
  matrix products  6.68 us (4%)
  other arithmetic  4.74 us (3%)
    all_to_all x1, waiting for transfers between devices, one_exchange(): parts = lax.all_to_all(parts, axis, split_axis=0, concat_axis=0, tiled=True)  47.7 us
    psum x3, blocking collectives, by_axis(): return functools.reduce(lax.psum, axes, array)  46 us
    all_to_all x1, starting transfers between devices, body(): lax.all_to_all(jnp.stack(jnp.split(beam_weights, lax.axis_size('sub'), ax...  44.9 us
    all_to_all x1, starting transfers between devices, one_exchange(): parts = lax.all_to_all(parts, axis, split_axis=0, concat_axis=0, tiled=True)  16.2 us
    reshape x2, local copies, waits for them, and re-layouts, body(): jnp.concatenate(lax.all_to_all(jnp.stack(jnp.split(beam_weights, lax.axis...  3.67 us
  transfers between devices with their start and end apart: 2, of which 1 were waited for; matrix products, arithmetic and copies ran while one was open for 5% of the time, Pallas kernels for 0%

profile of v1, /device:TPU:65, one launch (start us, length us, event | category | flops | bytes accessed | tf_op | source)
XLA Modules:
  0.0 180.6 jit_solution(14111805395530618673)
XLA Ops:
  0.6 1.3 slice_bitcast_fusion.3
  1.9 0.1 pad_maximum_fusion
  2.0 0.0 copy-start
  2.0 1.4 reshape.176
  3.4 44.9 %all-to-all-start.1 = ((f32[2,1,65536]{2,1,0:T(1,128)}), f32[2,1,65536]{2,1,0:T(1,128)S(1)}, u32[]{:S(2)}, u32[]{:S(2)}) async-start(f32[2,1,65536]{2,1,0:T(1,128)} %reshape.176), calls=%async_computation.1 | async-start | bytes 1048576 | tf_op jit(solution)/shard_map/all_to_all | solution.py:91
  48.4 0.0 copy-done
  48.4 1.3 copy.12
  49.7 0.0 all-to-all-done.1
  49.7 0.0 copy-start.1
  49.7 16.2 %all-to-all-start = ((f32[256,2,1,1,2,1,1,2,128]{8,7,4,1,6,5,3,2,0:T(2,128)}), f32[256,2,1,1,2,1,1,2,128]{8,7,4,1,6,5,3,2,0:T(2,128)S(1)}, u32[]{:S(2)}, u32[]{:S(2)}) async-start(f32[256,2,1,1,2,1,1,2,128]{8,7,4,1,6,5,3,2,0:T(2,128)} %bitcast.5), calls=%async_computation | async-start | bytes 2097152 | tf_op jit(solution)/shard_map/all_to_all | solution.py:34
  65.9 0.0 copy-done.1
  66.0 0.0 copy-start.2
  66.0 0.1 reshape.166
  66.1 0.6 copy-done.2
  66.7 0.5 broadcast.73
  67.2 2.3 %reduce.4 = f32[2,65536]{1,0:T(2,128)S(1)} reduce(f32[2,1,65536]{2,1,0:T(1,128)S(1)} %all-to-all-done.1, f32[]{:T(128)} %broadcast.73), dimensions={1}, to_apply=%all_to_all.7.reduce_sub_computation | reduce | bytes 1048580 | tf_op jit(solution)/shard_map/all_to_all | solution.py:91
  69.5 0.6 reshape.177
  70.1 1.9 %copy.16 = f32[1,8,2,64,2,64]{5,4,3,1,2,0:T(2,128)} copy(f32[1,8,2,64,2,64]{5,3,2,1,0,4:T(8,128)S(1)} %bitcast.100) | data formatting | bytes 1048576 | tf_op jit(solution)/shard_map/reshape | solution.py:90
  72.0 1.8 %reshape.161 = f32[1,8,2,64,128]{4,3,1,2,0:T(8,128)S(1)} reshape(f32[1,8,2,64,2,64]{5,4,3,1,2,0:T(2,128)} %copy.16) | data formatting | bytes 1048576 | tf_op jit(solution)/shard_map/reshape | solution.py:90
  73.8 0.1 broadcast_bitcast_fusion
  73.9 47.7 %all-to-all-done = f32[256,2,1,1,2,1,1,2,128]{8,7,4,1,6,5,3,2,0:T(2,128)S(1)} async-done(((f32[256,2,1,1,2,1,1,2,128]{8,7,4,1,6,5,3,2,0:T(2,128)}), f32[256,2,1,1,2,1,1,2,128]{8,7,4,1,6,5,3,2,0:T(2,128)S(1)}, u32[]{:S(2)}, u32[]{:S(2)}) %all-to-all-start) | async-done | bytes 1048608 | tf_op jit(solution)/shard_map/all_to_all | solution.py:34
  121.5 0.4 copy.13
  121.9 0.8 copy.14
  122.7 2.6 %gather_fusion = f32[512,2,256]{2,1,0:T(2,128)S(1)} fusion(f32[1,2,512,256]{3,1,2,0:T(2,128)S(1)} %copy.14, s32[512]{0:T(512)S(1)} %reshape.166), kind=kCustom, calls=%fused_computation | custom fusion | bytes 2101248 | tf_op jit(solution)/shard_map/vmap(jit(_take))/gather | solution.py:45
  125.3 0.1 copy.15
  125.4 0.1 broadcast_select_fusion
  125.5 0.6 fusion.12
  126.2 0.6 fusion.8
  126.8 0.6 fusion.2
  127.5 0.4 fusion.19
  127.8 0.4 fusion.18
  128.2 0.6 convolution_bitcast_fusion.2
  128.9 0.6 convolution_bitcast_fusion
  129.5 0.6 fusion.3
  130.1 0.4 fusion
  130.5 0.4 fusion.5
  131.0 0.6 fusion.6
  131.6 0.7 add_reduce_fusion
  132.3 0.1 stack.21
  132.4 0.1 stack.22
  132.5 20.4 %psum.21 = f32[128]{0:T(128)S(1)} all-reduce(f32[128]{0:T(128)S(1)} %get-tuple-element.5), channel_id=1, replica_groups=mesh['groups'=2,'range_0'=16,'range_1'=8,'sub'=2] {'range_0'}, use_global_device_ids=true, to_apply=%region_2.3 | all-reduce | flops 128 | bytes 1024 | tf_op jit(solution)/shard_map/psum | solution.py:40
  152.8 11.9 %psum.22 = f32[128]{0:T(128)S(1)} all-reduce(f32[128]{0:T(128)S(1)} %psum.21), channel_id=1, replica_groups=mesh['groups'=2,'range_0'=16,'range_1'=8,'sub'=2] {'range_1'}, use_global_device_ids=true, to_apply=%region_3.4 | all-reduce | flops 128 | bytes 1024 | tf_op jit(solution)/shard_map/psum | solution.py:40
  164.7 13.7 %psum.23 = f32[128]{0:T(128)S(1)} all-reduce(f32[128]{0:T(128)S(1)} %psum.22), channel_id=1, replica_groups=mesh['groups'=2,'range_0'=16,'range_1'=8,'sub'=2] {'sub'}, use_global_device_ids=true, to_apply=%region_4.5 | all-reduce | flops 128 | bytes 1024 | tf_op jit(solution)/shard_map/psum | solution.py:40
  178.4 0.5 broadcast_multiply_fusion.2
  178.9 0.8 pad_maximum_fusion.2
  179.8 0.8 pad_maximum_fusion.1
  (6 shorter events, 0.0 us)
Async XLA Ops:
  2.0 46.3 %copy-start = (f32[2,2,512,128]{3,2,1,0:T(8,128)S(1)}, f32[2,2,512,128]{3,2,1,0:T(8,128)}, u32[]{:S(2)}) copy-start(f32[2,2,512,128]{3,2,1,0:T(8,128)} %param.4) | copy-start | bytes 3145732
  3.4 46.3 %all-to-all-start.1 = ((f32[2,1,65536]{2,1,0:T(1,128)}), f32[2,1,65536]{2,1,0:T(1,128)S(1)}, u32[]{:S(2)}, u32[]{:S(2)}) async-start(f32[2,1,65536]{2,1,0:T(1,128)} %reshape.176), calls=%async_computation.1 | async-start | bytes 1048576 | tf_op jit(solution)/shard_map/all_to_all | solution.py:91
  49.7 16.2 %copy-start.1 = (s32[1,8,64]{2,1,0:T(8,128)S(1)}, s32[1,8,64]{2,1,0:T(8,128)}, u32[]{:S(2)}) copy-start(s32[1,8,64]{2,1,0:T(8,128)} %param.6) | copy-start | bytes 6148
  49.7 71.8 %all-to-all-start = ((f32[256,2,1,1,2,1,1,2,128]{8,7,4,1,6,5,3,2,0:T(2,128)}), f32[256,2,1,1,2,1,1,2,128]{8,7,4,1,6,5,3,2,0:T(2,128)S(1)}, u32[]{:S(2)}, u32[]{:S(2)}) async-start(f32[256,2,1,1,2,1,1,2,128]{8,7,4,1,6,5,3,2,0:T(2,128)} %bitcast.5), calls=%async_computation | async-start | bytes 2097152 | tf_op jit(solution)/shard_map/all_to_all | solution.py:34
  66.0 0.7 copy-start.2
